TPU v7x, 128 devices: a whole 4x4x4 slice. The times are simulated.
128 devices in a mesh: dp: 32 (over z, y, core), mp: 4 (over x).
Axes of the slice: x: 4, y: 4, z: 4, core: 2. Of those that a mesh axis runs over, the one named last changes fastest.
Arguments:
- queries: bfloat16 [1024, 64, 128], P('dp', 'mp'), may hold values from -8 to 8
- lookup_sheets: bfloat16 [32768, 16, 8, 128], P('dp', None, 'mp'), may hold values from -6 to 6
- content_sheets: bfloat16 [32768, 16, 8, 128], P('dp', None, 'mp'), may hold values from -12 to 12
- page_table: int32 [1024, 32], replicated, may hold values from 0 to 32767, as said below
- context_len: int32 [1024], replicated, may hold values from 32 to 512, as said below
- out_weight: bfloat16 [8192, 8192], P('mp', 'dp'), may hold values from -0.0625 to 0.0625
Outputs:
- attention: bfloat16 [1024, 64, 128], P('dp', 'mp')
- projected: bfloat16 [1024, 8192], P('mp', 'dp')
Inputs may be any that keep to these rules, and one draw needn't show every extreme that they name: `page_table`: every entry names a pool page, 0 to 32767, and every pool page appears exactly once in the whole table. `context_len`: each length lies between 32 and 512; most contexts are short, and some request has exactly 512 tokens.
All inputs are finite; a program needn't handle non-finite values.
Results may differ from a plain program's by a relative error of at most 0.0015.
Values may be sent and summed in bfloat16 or wider, within the bound.
A program may use at most 128 MiB of HBM per device.

v0:
```python
import functools

import jax
import jax.numpy as jnp
from jax import lax
from jax.experimental import pallas as pl
from jax.experimental.pallas import tpu as pltpu
from jax.sharding import PartitionSpec as P

MESH = pl.DeviceIdType.MESH
NEG = -1e30
RING = 4
LISTED = 2048
GROUP = 4
UNROLL = 8


def place():
    me = lax.axis_index("dp")
    return lax.rem(me, 2), lax.rem(me // 2, RING), me // (2 * RING)


def around(i):
    return lax.rem(i + RING, RING)


def spot(side, y, z):
    return (around(z) * RING + around(y)) * 2 + side


def remote(src, dst, send, recv, target):
    return pltpu.make_async_remote_copy(
        src_ref=src, dst_ref=dst, send_sem=send, recv_sem=recv,
        device_id=target, device_id_type=MESH,
    )


def greet(peers):
    barrier = pltpu.get_barrier_semaphore()
    for peer in peers:
        pl.semaphore_signal(barrier, inc=1, device_id=peer, device_id_type=MESH)
    pl.semaphore_wait(barrier, len(peers))


def near():
    side, y, z = place()
    return [
        {"dp": spot(side, y + 1, z)}, {"dp": spot(side, y - 1, z)},
        {"dp": spot(side, y, z + 1)}, {"dp": spot(side, y, z - 1)},
        {"dp": spot(1 - side, y, z)},
    ]


def torus_gather(view, send_sem, recv_sem, filler=None):
    side, y, z = place()
    sent = []

    def piece(q, i, j):
        return (side, y + i, z + j) if q < 2 else (side, y + j, z + i)

    def copy(q, what, target):
        at = view(q, *what)
        return remote(at, at, send_sem.at[len(sent)], recv_sem.at[spot(*what), q], {"dp": target})

    def send(q, what, target):
        out = copy(q, what, target)
        out.start()
        sent.append(out)

    def take(q, i, j, to=()):
        what = piece(q, i, j)
        if (i, j) != (0, 0):
            copy(q, what, spot(side, y, z)).wait_recv()
        for target in to:
            send(q, what, spot(*piece(q, *target)))
        send(q, what, spot(1 - side, y, z))

    both = ((0, 1), (0, -1))
    for q in range(4):
        take(q, 0, 0, ((1, 0), (-1, 0)) + both)
    if filler is not None:
        filler()
    stages = (
        (lambda d: (-d, 0), lambda d: ((d, 0),) + both),
        (lambda d: (d, 0), lambda d: both),
        (lambda d: (0, -d), lambda d: ((0, d),)),
        (lambda d: (0, d), lambda d: ()),
        (lambda d: (2, 0), lambda d: both),
        (lambda d: (-d, -d), lambda d: ((0, d),)),
        (lambda d: (d, -d), lambda d: ((0, d),)),
        (lambda d: (-d, d), lambda d: ()),
        (lambda d: (d, d), lambda d: ()),
        (lambda d: (0, 2), lambda d: ()),
        (lambda d: (2, -d), lambda d: ((0, d),)),
        (lambda d: (-d, 2), lambda d: ()),
        (lambda d: (d, 2), lambda d: ()),
        (lambda d: (2, d), lambda d: ()),
        (lambda d: (2, 2), lambda d: ()),
    )
    for where, to in stages:
        for q in range(4):
            d = 1 - 2 * (q % 2)
            take(q, *where(d), to(d))
    for i in range(RING):
        for j in range(RING):
            for q in range(4):
                copy(q, (1 - side, i, j), spot(side, y, z)).wait_recv()
    for out in sent:
        out.wait_send()


def torus_sems():
    n = lax.axis_size("dp")
    dma = pltpu.SemaphoreType.DMA
    return [dma((124,)), dma((n, 4))]


def plan(sizes, table_ref, len_ref, list_ref, pos_ref, code_ref):
    pool_local, page_len = sizes
    slots, rows = table_ref.shape
    f32, bf16, i32 = jnp.float32, jnp.bfloat16, jnp.int32

    def iota(shape, dim):
        return lax.broadcasted_iota(i32, shape, dim)

    def ones(mask):
        return jnp.where(mask, 1.0, 0.0)

    local = table_ref[...] - lax.axis_index("dp") * pool_local
    used = jnp.clip(len_ref[...] - iota((slots, rows), 0) * page_len, 0, page_len)
    wanted = (local >= 0) & (local < pool_local) & (used > 0)
    flags = ones(wanted)
    lower = ones(iota((slots, slots), 1) < iota((slots, slots), 0)).astype(bf16)
    rank = jnp.dot(lower, flags.astype(bf16), preferred_element_type=f32)
    count = jnp.sum(flags, axis=0, keepdims=True)
    some = jnp.minimum(count, 1.0)
    extra = jnp.maximum(count - 1.0, 0.0)
    both = jnp.where(iota((8, rows), 0) == 0, some, extra).astype(bf16)
    upper = ones(iota((rows, rows), 0) < iota((rows, rows), 1)).astype(bf16)
    ahead = jnp.dot(both, upper, preferred_element_type=f32)
    pos = jnp.where(rank == 0.0, ahead[0:1], (LISTED - 1) - ahead[1:2] - (rank - 1.0))
    pos_ref[...] = jnp.where(wanted, pos, -1.0).astype(i32)

    t = iota((1, rows), 1)
    q, turn, y, z = (t >> 3) & 3, (t >> 5) & 1, (t >> 6) & 3, (t >> 8) & 3
    f = jnp.where(q < 2, y, z)
    g = jnp.where(q < 2, z, y)
    row = (q << 8) | (f << 6) | (turn << 5) | (g << 3) | (t & 7)
    code_ref[...] = jnp.where(wanted, (row << 15) | (local << 5) | used, 0)

    high = iota((LISTED // 128, rows), 0)
    low = iota((128, rows), 0)

    def collect(s, total):
        p = pos_ref[pl.ds(s, 1)]
        c = code_ref[pl.ds(s, 1)]
        hit = high == (p >> 7)
        bytes_of = [jnp.where(hit, ((c >> (8 * k)) & 255).astype(f32), 0.0) for k in range(4)]
        left = jnp.concatenate(bytes_of, axis=0).astype(bf16)
        right = ones(low == (p & 127)).astype(bf16)
        return total + lax.dot_general(
            left, right, (((1,), (1,)), ((), ())), preferred_element_type=f32
        )

    height = LISTED // 128
    total = lax.fori_loop(0, slots, collect, jnp.zeros((4 * height, 128), f32)).astype(i32)
    out = total[:height]
    for k in range(1, 4):
        out = out + total[k * height : (k + 1) * height] * (1 << (8 * k))
    list_ref[0:height] = jnp.where(out == 0, rows << 15, out)
    sums = jnp.where(
        iota((8, 128), 0) == 0, jnp.sum(some, axis=1, keepdims=True),
        jnp.sum(extra, axis=1, keepdims=True),
    )
    list_ref[height : height + 8] = sums.astype(i32)


def gather_kernel(
    sizes, q_ref, table_ref, len_ref, all_ref, list_ref, pos_ref, code_ref, own_sem, send, recv
):
    side, y, z = place()

    def view(q, of, at_y, at_z):
        f, g = (at_y, at_z) if q < 2 else (at_z, at_y)
        return all_ref.at[q, around(f), of, around(g)]

    own = [
        pltpu.make_async_copy(q_ref.at[q], view(q, side, y, z), own_sem.at[q]) for q in range(4)
    ]
    for copy in own:
        copy.start()
    greet(near())
    for copy in own:
        copy.wait()
    torus_gather(
        view, send, recv,
        lambda: plan(sizes, table_ref, len_ref, list_ref, pos_ref, code_ref),
    )


def gather_queries(queries, table, lengths, sizes):
    rows, q_local, head_dim = queries.shape
    dma = pltpu.SemaphoreType.DMA
    vmem = pl.BlockSpec(memory_space=pltpu.VMEM)
    return pl.pallas_call(
        functools.partial(gather_kernel, sizes),
        out_shape=(
            jax.ShapeDtypeStruct((4, RING, 2, RING, rows // 4, q_local, head_dim), queries.dtype),
            jax.ShapeDtypeStruct((LISTED // 128 + 8, 128), jnp.int32),
        ),
        in_specs=[vmem] * 3,
        out_specs=(vmem, vmem),
        scratch_shapes=[
            pltpu.VMEM(table.shape, jnp.int32), pltpu.VMEM(table.shape, jnp.int32), dma((4,)),
        ] + torus_sems(),
        compiler_params=pltpu.CompilerParams(collective_id=0, has_side_effects=True, vmem_limit_bytes=8 << 20),
        cost_estimate=pl.CostEstimate(flops=20_000_000_000, bytes_accessed=8 << 20, transcendentals=0),
    )(queries.reshape(4, rows // 4, q_local, head_dim), table, lengths)


def attend_kernel(
    sizes, listed, q_ref, kbuf, vbuf, acc_turned, stat_turned,
    acc_ref, stat_ref,
):
    kv_local, blocks = sizes
    rows, q_local, head_dim = q_ref.shape
    pages, span, _ = kbuf.shape
    f32, i32 = jnp.float32, jnp.int32
    tall = GROUP * q_local
    wide = GROUP * span
    whole_lane = lax.broadcasted_iota(i32, (128, 128), 1)

    @pl.loop(0, blocks)
    def _(b):
        acc_ref[b] = jnp.zeros(acc_ref.shape[1:], f32)
        stat_ref[b] = jnp.where(whole_lane % 2 == 0, NEG, 0.0)

    lane = lax.broadcasted_iota(i32, (tall, wide), 1)
    line = lax.broadcasted_iota(i32, (tall, wide), 0)
    fits = (lane // span == line // q_local) & (
        lane % kv_local == (line % q_local) // (q_local // kv_local)
    )
    token = jnp.where(fits, (lane % span) // kv_local, 64)
    stat_lane = lax.broadcasted_iota(i32, (q_local, 128), 1)
    scale = head_dim ** (-0.5)

    def half(first):
        codes = [listed[first + i] for i in range(GROUP)]
        used = [code & 31 for code in codes]
        page = [(code >> 5) & (pages - 1) for code in codes]
        row = [code >> 15 for code in codes]
        asked = jnp.concatenate([q_ref[r & (rows - 1)] for r in row], axis=0)
        keys = jnp.concatenate([kbuf[p] for p in page], axis=0)
        values = jnp.concatenate([vbuf[p] for p in page], axis=0)
        limit = jnp.concatenate([jnp.full((q_local, wide), u, i32) for u in used], axis=0)
        return row, asked, keys, values, token < limit

    def soft(scores, valid):
        scores = jnp.where(valid, scores * scale, NEG)
        peak = jnp.max(scores, axis=1, keepdims=True)
        weights = jnp.where(valid, jnp.exp(scores - peak), 0.0)
        return peak, jnp.sum(weights, axis=1, keepdims=True), weights.astype(jnp.bfloat16)

    def quad(firsts):
        halves = [half(first) for first in firsts]
        scores = [
            lax.dot_general(h[1], h[2], (((1,), (1,)), ((), ())), preferred_element_type=f32)
            for h in halves
        ]
        soft_of = [soft(x, h[4]) for x, h in zip(scores, halves)]
        none = jnp.zeros((tall, wide), jnp.bfloat16)
        left = jnp.concatenate([
            jnp.concatenate([x[2], none] if k % 2 == 0 else [none, x[2]], axis=1)
            for k, x in enumerate(soft_of)
        ], axis=0)
        right = jnp.concatenate([
            jnp.concatenate([halves[k][3], halves[k + 1][3]], axis=0)
            for k in range(0, len(halves), 2)
        ], axis=1)
        acc = jnp.dot(left, right, preferred_element_type=f32)
        out = []
        for k in range(len(halves)):
            part = acc[k * tall : (k + 1) * tall, (k // 2) * head_dim : (k // 2 + 1) * head_dim]
            for i in range(GROUP):
                at = slice(i * q_local, (i + 1) * q_local)
                out.append((halves[k][0][i], soft_of[k][0][at], soft_of[k][1][at], part[at]))
        return out

    def split(row):
        first = pl.multiple_of((row & 7) * q_local, q_local)
        peak_here = stat_lane == ((row >> 3) & 3) * 2
        mass_here = stat_lane == ((row >> 3) & 3) * 2 + 1
        return row >> 5, row & 31, pl.ds(first, q_local), peak_here, mass_here

    first_count = listed[LISTED]
    more_count = listed[LISTED + 128]
    step = GROUP * UNROLL

    @pl.loop(0, (first_count + step - 1) // step)
    def _(i):
        parts = []
        for u in range(0, UNROLL, 4):
            parts += quad([i * step + (u + k) * GROUP for k in range(4)])
        for row, peak, mass, acc in parts:
            block, at, lines, peak_here, mass_here = split(row)
            acc_ref[block, at] = acc
            stat_ref[block, lines] = jnp.where(
                peak_here, peak, jnp.where(mass_here, mass, stat_ref[block, lines])
            )

    @pl.loop(0, (more_count + 2 * GROUP - 1) // (2 * GROUP))
    def _(i):
        parts = quad([LISTED - GROUP - i * 2 * GROUP, LISTED - 2 * GROUP - i * 2 * GROUP])
        for row, peak, mass, acc in parts:
            block, at, lines, peak_here, mass_here = split(row)
            old = stat_ref[block, lines]
            old_peak = jnp.max(jnp.where(peak_here, old, NEG), axis=1, keepdims=True)
            old_mass = jnp.sum(jnp.where(mass_here, old, 0.0), axis=1, keepdims=True)
            top = jnp.maximum(old_peak, peak)
            old_f = jnp.exp(old_peak - top)
            new_f = jnp.exp(peak - top)
            acc_ref[block, at] = acc_ref[block, at] * old_f + acc * new_f
            stat_ref[block, lines] = jnp.where(
                peak_here, top, jnp.where(mass_here, old_mass * old_f + mass * new_f, old)
            )

    eighth = 128 // q_local

    @pl.loop(0, blocks - 1)
    def _(b):
        for g in range(4):
            tile = acc_ref[b, g * eighth : (g + 1) * eighth].reshape(128, head_dim)
            acc_turned[b, g] = tile.T
        stat_turned[b] = stat_ref[b].T[:8]


def attend(listed, queries, keys, values, kv_local):
    rows, q_local, head_dim = queries.shape
    blocks = rows // 32 + 1
    f32 = jnp.float32
    vmem = pl.BlockSpec(memory_space=pltpu.VMEM)
    return pl.pallas_call(
        functools.partial(attend_kernel, (kv_local, blocks)),
        out_shape=(
            jax.ShapeDtypeStruct((blocks - 1, 4, head_dim, 128), f32),
            jax.ShapeDtypeStruct((blocks - 1, 8, 128), f32),
        ),
        in_specs=[pl.BlockSpec(memory_space=pltpu.SMEM), vmem, vmem, vmem],
        out_specs=(vmem, vmem),
        scratch_shapes=[
            pltpu.VMEM((blocks, 32, q_local, head_dim), f32),
            pltpu.VMEM((blocks, 128, 128), f32),
        ],
        compiler_params=pltpu.CompilerParams(vmem_limit_bytes=16 << 20),
    )(listed, queries, keys, values)


def finish_kernel(
    acc_hbm, stat_hbm, w_hbm, att_out, proj_out,
    got_acc, got_stat, out_code, out_stat, in_code, in_stat,
    last_code, last_stat, weight, mixed, everyone, part_out, part_step_out, part_in, part_step_in,
    cross_send, cross_recv, hop_send, hop_recv, last_send, last_recv, w_sem,
    part_send, part_recv,
    torus_send, torus_recv,
):
    n = lax.axis_size("dp")
    me = lax.axis_index("dp")
    m = lax.axis_size("mp")
    mine = lax.axis_index("mp")
    side, y, z = place()
    rows, q_local, head_dim = att_out.shape
    out_rows = proj_out.shape[0]
    half_width = proj_out.shape[1] // 2
    f32 = jnp.float32
    load_w = pltpu.make_async_copy(w_hbm, weight, w_sem)
    load_w.start()

    def axes(q):
        return jnp.where(q < 2, y, z), jnp.where(q < 2, z, y), 1 - 2 * lax.rem(q, 2)

    def first_axis(q, i):
        return {"dp": jnp.where(q < 2, spot(side, y + i, z), spot(side, y, z + i))}

    def second_axis(q, i):
        return {"dp": jnp.where(q < 2, spot(side, y, z + i), spot(side, y + i, z))}

    def block_of(kind, q, of):
        f, _, d = axes(q)
        f = around(f + jnp.where(kind == 0, 2, jnp.where(kind == 1, -d, jnp.where(kind == 2, d, 0))))
        return (q * RING + f) * 2 + of

    def cross_copies(kind, q):
        at = block_of(kind, q, 1 - side)
        peer = {"dp": spot(1 - side, y, z)}
        return (
            remote(acc_hbm.at[at], got_acc.at[kind, q], cross_send.at[0, kind, q],
                   cross_recv.at[0, kind, q], peer),
            remote(stat_hbm.at[at], got_stat.at[kind, q], cross_send.at[1, kind, q],
                   cross_recv.at[1, kind, q], peer),
        )

    def hop_copies(kind, q):
        _, _, d = axes(q)
        peer = first_axis(q, jnp.where(kind == 1, -d, d))
        return (
            remote(out_code.at[kind, q], in_code.at[kind, q], hop_send.at[0, kind, q],
                   hop_recv.at[0, kind, q], peer),
            remote(out_stat.at[kind, q], in_stat.at[kind, q], hop_send.at[1, kind, q],
                   hop_recv.at[1, kind, q], peer),
        )

    def last_copies(o, q):
        _, g, _ = axes(q)
        peer = second_axis(q, o)
        at = around(g + o)
        return (
            remote(out_code.at[3, q, at], last_code.at[o - 1, q],
                   last_send.at[0, o - 1, q], last_recv.at[0, o - 1, q], peer),
            remote(out_stat.at[3, q, at], last_stat.at[o - 1, q],
                   last_send.at[1, o - 1, q], last_recv.at[1, o - 1, q], peer),
        )

    peers = near() + [{"dp": spot(side, y + 2, z)}, {"dp": spot(side, y, z + 2)}]
    peers += [{"mp": lax.rem(mine + i, m)} for i in range(1, m)]
    greet(peers)

    @pl.loop(0, 16)
    def _(i):
        for copy in cross_copies(i // 4, lax.rem(i, 4)):
            copy.start()

    def combine(parts):
        top = parts[0][0]
        for part in parts[1:]:
            top = jnp.maximum(top, part[0])
        mass = 0.0
        gains = []
        for its_top, its_mass, step in parts:
            factor = jnp.exp(its_top - top)
            mass = mass + factor * its_mass
            gains.append(factor if step is None else factor * step)
        return top, mass, gains

    def coded(tile):
        return tile[0:1], tile[1:2], tile[2:3]

    def encode(value):
        step = jnp.max(jnp.abs(value), axis=0, keepdims=True) * (1.0 / 32767.0)
        floor = jnp.maximum(step, 1e-30)
        inverse = 1.0 / floor
        inverse = jnp.where(step > 1e-30, inverse * (2.0 - floor * inverse), 0.0)
        return jnp.round(value * inverse).astype(jnp.int32).astype(jnp.int16), step

    def gathered(kind, q, arrived):
        own = block_of(kind, q, side)
        for copy in cross_copies(kind, q):
            copy.wait_recv()
        for other in arrived:
            for copy in hop_copies(other, q):
                copy.wait_recv()
        for g in range(4):
            plain = [
                (stat[2 * g : 2 * g + 1], stat[2 * g + 1 : 2 * g + 2], None)
                for stat in (stat_hbm[own], got_stat[kind, q])
            ]
            top, mass, gains = combine(plain + [coded(in_stat[k, q, g]) for k in arrived])
            value = acc_hbm[own, g] * gains[0] + got_acc[kind, q, g] * gains[1]
            for gain, k in zip(gains[2:], arrived):
                value = value + in_code[k, q, g].astype(f32) * gain
            out_code[kind, q, g], step = encode(value)
            out_stat[kind, q, g, 0:1] = top
            out_stat[kind, q, g, 1:2] = mass
            out_stat[kind, q, g, 2:3] = step

    @pl.loop(0, 8)
    def _(i):
        kind, q = i // 4, lax.rem(i, 4)
        gathered(kind, q, ())
        for copy in hop_copies(kind, q):
            copy.start()

    @pl.loop(0, 4)
    def _(q):
        gathered(2, q, (0,))
        for copy in hop_copies(2, q):
            copy.start()

    @pl.loop(0, 4)
    def _(q):
        gathered(3, q, (1, 2))
        for o in (1, 3, 2):
            for copy in last_copies(o, q):
                copy.start()

    @pl.loop(0, 4)
    def _(q):
        _, g, _ = axes(q)
        parts = [coded(out_stat[3, q, g])]
        for o in range(1, 4):
            for copy in last_copies(o, q):
                copy.wait_recv()
            parts.append(coded(last_stat[o - 1, q]))
        _, mass, gains = combine(parts)
        value = out_code[3, q, g].astype(f32) * (gains[0] / mass)
        for o in range(1, 4):
            value = value + last_code[o - 1, q].astype(f32) * (gains[o] / mass)
        mixed[pl.ds(q * (rows // 4), rows // 4)] = value.T.reshape(rows // 4, q_local, head_dim)

    att_out[...] = mixed[...].astype(jnp.bfloat16)
    for h in range(q_local):
        at = (h % 4) * head_dim
        everyone[me, h // 4, :, at : at + head_dim] = mixed[:, h, :].astype(jnp.bfloat16)

    torus_gather(lambda q, of, at_y, at_z: everyone.at[spot(of, at_y, at_z), q], torus_send, torus_recv)
    load_w.wait()

    band = q_local * head_dim // 4
    homes = n // m

    def rows_of(i):
        at = pl.multiple_of(lax.rem(mine + i + m, m) * homes, homes)
        value = 0.0
        for q in range(4):
            value += jnp.dot(
                everyone[pl.ds(at, homes), q].reshape(out_rows, band),
                weight[q * band : (q + 1) * band], preferred_element_type=f32,
            )
        return value

    def side_copies(kind, half):
        by = 1 - 2 * half
        peer = {"mp": lax.rem(mine + (m - by if kind == 1 else by) + m, m)}
        return (
            remote(part_out.at[kind, half], part_in.at[kind, half], part_send.at[0, kind, half],
                   part_recv.at[0, kind, half], peer),
            remote(part_step_out.at[kind, half], part_step_in.at[kind, half],
                   part_send.at[1, kind, half], part_recv.at[1, kind, half], peer),
        )

    def put(kind, half, value):
        part_out[kind, half], step = encode(value)
        part_step_out[kind, half, 0:1] = step
        for copy in side_copies(kind, half):
            copy.start()

    def arrived(kind, half):
        for copy in side_copies(kind, half):
            copy.wait_recv()
        return part_in[kind, half].astype(f32) * part_step_in[kind, half, 0:1]

    halves = [slice(0, half_width), slice(half_width, 2 * half_width)]
    value = rows_of(2)
    for half in range(2):
        put(0, half, value[:, halves[half]])
    before = rows_of(-1)
    put(1, 0, before[:, halves[0]])
    after = rows_of(1)
    put(1, 1, after[:, halves[1]])
    put(2, 0, after[:, halves[0]] + arrived(0, 0))
    put(2, 1, before[:, halves[1]] + arrived(0, 1))
    value = rows_of(0)
    for half in range(2):
        total = value[:, halves[half]] + arrived(1, half) + arrived(2, half)
        proj_out[:, halves[half]] = total.astype(jnp.bfloat16)
    for kind in range(3):
        for half in range(2):
            for copy in side_copies(kind, half):
                copy.wait_send()

    @pl.loop(0, 16)
    def _(i):
        for copy in cross_copies(i // 4, lax.rem(i, 4)):
            copy.wait_send()

    @pl.loop(0, 12)
    def _(i):
        kind, q = i // 4, lax.rem(i, 4)
        for copy in hop_copies(kind, q) + last_copies(kind + 1, q):
            copy.wait_send()


def finish(acc, stat, out_weight, q_local):
    _, _, head_dim, _ = acc.shape
    rows = 4 * 128 // q_local
    n = lax.axis_size("dp")
    m = lax.axis_size("mp")
    depth, columns = out_weight.shape
    out_rows = n * rows // m
    dma = pltpu.SemaphoreType.DMA
    f32, i16 = jnp.float32, jnp.int16
    return pl.pallas_call(
        finish_kernel,
        out_shape=(
            jax.ShapeDtypeStruct((rows, q_local, head_dim), jnp.bfloat16),
            jax.ShapeDtypeStruct((out_rows, columns), jnp.bfloat16),
        ),
        in_specs=[pl.BlockSpec(memory_space=pltpu.VMEM)] * 2 + [pl.BlockSpec(memory_space=pl.ANY)],
        out_specs=(pl.BlockSpec(memory_space=pltpu.VMEM),) * 2,
        scratch_shapes=[
            pltpu.VMEM((4, 4, 4, head_dim, 128), f32),
            pltpu.VMEM((4, 4, 8, 128), f32),
            pltpu.VMEM((4, 4, 4, head_dim, 128), i16),
            pltpu.VMEM((4, 4, 4, 4, 128), f32),
            pltpu.VMEM((3, 4, 4, head_dim, 128), i16),
            pltpu.VMEM((3, 4, 4, 4, 128), f32),
            pltpu.VMEM((3, 4, head_dim, 128), i16),
            pltpu.VMEM((3, 4, 4, 128), f32),
            pltpu.VMEM((depth, columns), out_weight.dtype),
            pltpu.VMEM((rows, q_local, head_dim), f32),
            pltpu.VMEM((n, 4, rows, q_local * head_dim // 4), jnp.bfloat16),
            pltpu.VMEM((3, 2, out_rows, columns // 2), i16),
            pltpu.VMEM((3, 2, 8, columns // 2), f32),
            pltpu.VMEM((3, 2, out_rows, columns // 2), i16),
            pltpu.VMEM((3, 2, 8, columns // 2), f32),
            dma((2, 4, 4)), dma((2, 4, 4)),
            dma((2, 3, 4)), dma((2, 3, 4)), dma((2, 3, 4)), dma((2, 3, 4)), dma,
            dma((2, 3, 2)), dma((2, 3, 2)),
        ] + torus_sems(),
        compiler_params=pltpu.CompilerParams(collective_id=1, has_side_effects=True, vmem_limit_bytes=24 << 20),
    )(acc, stat, out_weight)


def shards(queries, lookup_sheets, content_sheets, page_table, context_len, out_weight):
    req_rows = page_table.shape[0]
    pool_local, page_len, kv_local, head_dim = lookup_sheets.shape
    span = page_len * kv_local
    all_queries, listed = gather_queries(
        queries, page_table.T, context_len.reshape(1, req_rows), (pool_local, page_len)
    )
    acc, stat = attend(
        listed.reshape(-1), all_queries.reshape(req_rows, *queries.shape[1:]),
        lookup_sheets.reshape(pool_local, span, head_dim),
        content_sheets.reshape(pool_local, span, head_dim), kv_local,
    )
    return finish(acc, stat, out_weight, queries.shape[1])


def solution(mesh):
    placed = (
        P("dp", "mp", None),
        P("dp", None, "mp", None),
        P("dp", None, "mp", None),
        P(),
        P(),
        P("mp", "dp"),
    )
    return jax.shard_map(
        shards,
        mesh=mesh,
        in_specs=placed,
        out_specs=(P("dp", "mp", None), P("mp", "dp")),
        check_vma=False,
    )
```

profile of v0, /device:TPU:4, one launch (start us, length us, event | category | flops | bytes accessed | tf_op | source)
XLA Modules:
  0.0 103.4 jit_solution(9866741627939713159)
XLA Ops:
  0.6 0.0 copy-start.3
  0.6 0.9 copy-done.3
  1.5 0.0 copy-start.4
  1.5 0.9 copy-done.4
  2.4 0.0 copy-start.5
  2.4 0.7 copy-done.5
  3.1 0.0 copy-start
  3.1 0.0 copy-start.1
  3.1 27.8 %shard_map.77 = (bf16[4,4,2,4,8,16,128]{6,5,4,3,2,1,0:T(8,128)(2,1)S(1)}, s32[24,128]{1,0:T(8,128)S(1)}) custom-call(bf16[4,8,16,128]{3,2,1,0:T(8,128)(2,1)S(1)} %bitcast.11, s32[32,1024]{1,0:T(8,128)S(1)} %bitcast.12, s32[1,1024]{1,0:T(1,128)S(1)} %bitcast.13), custom_call_target="tpu_custom_call" | custom-call | flops 20000000000 | bytes 8388608 | tf_op jit(solution)/shard_map/pallas_call | solution.py:205
  31.0 0.0 copy-done
  31.0 0.0 copy-done.1
  31.0 0.0 copy-start.2
  31.0 20.1 %shard_map.78 = (f32[32,4,128,128]{3,2,1,0:T(8,128)S(1)}, f32[32,8,128]{2,1,0:T(8,128)S(1)}) custom-call(s32[3072]{0:T(1024)S(1)} %bitcast.10, bf16[1024,16,128]{2,1,0:T(8,128)(2,1)S(1)} %bitcast.9, bf16[1024,32,128]{2,1,0:T(8,128)(2,1)S(1)} %bitcast.7, bf16[1024,32,128]{2,1,0:T(8,128)(2,1)S(1)} %bitcast.8), custom_call_target="tpu_custom_call" | custom-call | tf_op jit(solution)/shard_map/pallas_call | solution.py:342
  51.1 0.0 copy-done.2
  51.1 51.0 %shard_map.79 = (bf16[32,16,128]{2,1,0:T(8,128)(2,1)S(1)}, bf16[256,256]{1,0:T(8,128)(2,1)S(1)}) custom-call(f32[32,4,128,128]{3,2,1,0:T(8,128)S(1)} %get-tuple-element.8.acc_hbm, f32[32,8,128]{2,1,0:T(8,128)S(1)} %get-tuple-element.9.stat_hbm, bf16[2048,256]{1,0:T(8,128)(2,1)S(1)} %copy-done.2), custom_call_target="tpu_custom_call" | custom-call | tf_op jit(solution)/shard_map/pallas_call | solution.py:591
  102.1 0.7 copy.10
  102.7 0.7 copy.11
Async XLA Ops:
  0.6 0.9 copy-start.3
  1.5 0.9 copy-start.4
  2.4 0.7 copy-start.5
  3.1 27.8 %copy-start = (bf16[1024,16,2,128]{3,2,1,0:T(2,128)(2,1)S(1)}, bf16[1024,16,2,128]{3,2,1,0:T(2,128)(2,1)}, u32[]{:S(2)}) copy-start(bf16[1024,16,2,128]{3,2,1,0:T(2,128)(2,1)} %param.7) | copy-start | bytes 25165828
  3.1 27.9 %copy-start.1 = (bf16[1024,16,2,128]{3,2,1,0:T(2,128)(2,1)S(1)}, bf16[1024,16,2,128]{3,2,1,0:T(2,128)(2,1)}, u32[]{:S(2)}) copy-start(bf16[1024,16,2,128]{3,2,1,0:T(2,128)(2,1)} %param.8) | copy-start | bytes 25165828
  31.0 20.1 %copy-start.2 = (bf16[2048,256]{1,0:T(8,128)(2,1)S(1)}, bf16[2048,256]{1,0:T(8,128)(2,1)}, u32[]{:S(2)}) copy-start(bf16[2048,256]{1,0:T(8,128)(2,1)} %w_hbm.1) | copy-start | bytes 3145732
where the time goes:
time: 105 us; the launch traced here: 103 us
  Pallas kernels  98.9 us (94%)
  local copies, waits for them, and re-layouts  3.81 us (4%)
    pallas_call x1, Pallas kernels, finish(): pl.pallas_call(finish_kernel, out_shape=(jax.ShapeDtypeStruct((rows, q_lo...  51 us
    pallas_call x1, Pallas kernels, gather_queries(): pl.pallas_call(functools.partial(gather_kernel, sizes), out_shape=(jax.Sh...  27.8 us
    pallas_call x1, Pallas kernels, attend(): pl.pallas_call(functools.partial(attend_kernel, (kv_local, blocks)), out_...  20.1 us
    unnamed x14, local copies, waits for them, and re-layouts  3.81 us

commit v1 on v0

--- a/solution.py
+++ b/solution.py
@@ -10,9 +10,12 @@
 MESH = pl.DeviceIdType.MESH
 NEG = -1e30
 RING = 4
-LISTED = 2048
+LISTED = 4096
+SECOND = 4096
+THIRD = 1536
+LATER = 2080
+BATCH = 32
 GROUP = 4
-UNROLL = 8
 
 
 def place():
@@ -51,8 +54,9 @@
     ]
 
 
-def torus_gather(view, send_sem, recv_sem, filler=None):
+def torus_gather(view, send_sem, recv_sem, between):
     side, y, z = place()
+    here = spot(side, y, z)
     sent = []
 
     def piece(q, i, j):
@@ -62,49 +66,64 @@
         at = view(q, *what)
         return remote(at, at, send_sem.at[len(sent)], recv_sem.at[spot(*what), q], {"dp": target})
 
-    def send(q, what, target):
-        out = copy(q, what, target)
+    def send(q, at, to):
+        out = copy(q, piece(q, *at), spot(*piece(q, *to)))
         out.start()
         sent.append(out)
 
-    def take(q, i, j, to=()):
-        what = piece(q, i, j)
-        if (i, j) != (0, 0):
-            copy(q, what, spot(side, y, z)).wait_recv()
-        for target in to:
-            send(q, what, spot(*piece(q, *target)))
-        send(q, what, spot(1 - side, y, z))
+    def take(*wheres):
+        for where, to in wheres:
+            for q in range(4):
+                d = 1 - 2 * (q % 2)
+                at = where(d)
+                copy(q, piece(q, *at), here).wait_recv()
+                for target in to(d):
+                    send(q, at, target)
+
+    def cross(*wheres):
+        for where in wheres:
+            for q in range(4):
+                what = piece(q, *where(1 - 2 * (q % 2)))
+                out = copy(q, what, spot(1 - side, y, z))
+                out.start()
+                sent.append(out)
+
+    def plane(j):
+        for i in range(RING):
+            for q in range(4):
+                copy(q, (1 - side, i, z + j), here).wait_recv()
 
     both = ((0, 1), (0, -1))
     for q in range(4):
-        take(q, 0, 0, ((1, 0), (-1, 0)) + both)
-    if filler is not None:
-        filler()
-    stages = (
-        (lambda d: (-d, 0), lambda d: ((d, 0),) + both),
-        (lambda d: (d, 0), lambda d: both),
-        (lambda d: (0, -d), lambda d: ((0, d),)),
-        (lambda d: (0, d), lambda d: ()),
-        (lambda d: (2, 0), lambda d: both),
-        (lambda d: (-d, -d), lambda d: ((0, d),)),
-        (lambda d: (d, -d), lambda d: ((0, d),)),
-        (lambda d: (-d, d), lambda d: ()),
-        (lambda d: (d, d), lambda d: ()),
-        (lambda d: (0, 2), lambda d: ()),
-        (lambda d: (2, -d), lambda d: ((0, d),)),
-        (lambda d: (-d, 2), lambda d: ()),
-        (lambda d: (d, 2), lambda d: ()),
-        (lambda d: (2, d), lambda d: ()),
-        (lambda d: (2, 2), lambda d: ()),
-    )
-    for where, to in stages:
-        for q in range(4):
-            d = 1 - 2 * (q % 2)
-            take(q, *where(d), to(d))
-    for i in range(RING):
-        for j in range(RING):
-            for q in range(4):
-                copy(q, (1 - side, i, j), spot(side, y, z)).wait_recv()
+        for to in ((1, 0), (-1, 0)):
+            send(q, (0, 0), to)
+    for q in range(4):
+        for to in both:
+            send(q, (0, 0), to)
+    cross(lambda d: (0, 0))
+    between(0, plane)
+    near_back, near_front = lambda d: (-d, 0), lambda d: (d, 0)
+    low, high = lambda d: (0, -d), lambda d: (0, d)
+    take((near_back, lambda d: ((d, 0),) + both), (low, lambda d: ((0, d),)))
+    take((near_front, lambda d: both), (high, lambda d: ()))
+    cross(near_back, low, near_front, high)
+    between(1, plane)
+    far = lambda d: (2, 0)
+    take((far, lambda d: both))
+    corners = [lambda d: (-d, -d), lambda d: (d, -d), lambda d: (-d, d), lambda d: (d, d)]
+    take((corners[0], lambda d: ((0, d),)), (corners[1], lambda d: ((0, d),)))
+    over = lambda d: (0, 2)
+    take((over, lambda d: ()), (corners[2], lambda d: ()), (corners[3], lambda d: ()))
+    cross(far, over, *corners)
+    between(2, plane)
+    take((lambda d: (2, -d), lambda d: ((0, d),)))
+    rest = [lambda d: (2, d), lambda d: (-d, 2), lambda d: (d, 2)]
+    take(*[(where, lambda d: ()) for where in rest])
+    cross(lambda d: (2, -d), *rest)
+    between(3, plane)
+    take((lambda d: (2, 2), lambda d: ()))
+    cross(lambda d: (2, 2))
+    between(4, plane)
     for out in sent:
         out.wait_send()
 
@@ -115,7 +134,7 @@
     return [dma((124,)), dma((n, 4))]
 
 
-def plan(sizes, table_ref, len_ref, list_ref, pos_ref, code_ref):
+def plan_start(sizes, table_ref, len_ref, list_ref, pos_ref, code_ref, total_ref):
     pool_local, page_len = sizes
     slots, rows = table_ref.shape
     f32, bf16, i32 = jnp.float32, jnp.bfloat16, jnp.int32
@@ -133,12 +152,16 @@
     lower = ones(iota((slots, slots), 1) < iota((slots, slots), 0)).astype(bf16)
     rank = jnp.dot(lower, flags.astype(bf16), preferred_element_type=f32)
     count = jnp.sum(flags, axis=0, keepdims=True)
-    some = jnp.minimum(count, 1.0)
-    extra = jnp.maximum(count - 1.0, 0.0)
-    both = jnp.where(iota((8, rows), 0) == 0, some, extra).astype(bf16)
+    line = iota((8, rows), 0)
+    held = jnp.maximum(count - line.astype(f32), 0.0)
+    held = jnp.where(line < 3, jnp.minimum(held, 1.0), jnp.where(line == 3, held, 0.0))
     upper = ones(iota((rows, rows), 0) < iota((rows, rows), 1)).astype(bf16)
-    ahead = jnp.dot(both, upper, preferred_element_type=f32)
-    pos = jnp.where(rank == 0.0, ahead[0:1], (LISTED - 1) - ahead[1:2] - (rank - 1.0))
+    ahead = jnp.dot(held.astype(bf16), upper, preferred_element_type=f32)
+    pos = jnp.where(
+        rank < 2.0,
+        jnp.where(rank == 0.0, ahead[0:1], SECOND - 1 - ahead[1:2]),
+        jnp.where(rank == 2.0, THIRD + ahead[2:3], LATER - 3 + rank + ahead[3:4]),
+    )
     pos_ref[...] = jnp.where(wanted, pos, -1.0).astype(i32)
 
     t = iota((1, rows), 1)
@@ -147,36 +170,44 @@
     g = jnp.where(q < 2, z, y)
     row = (q << 8) | (f << 6) | (turn << 5) | (g << 3) | (t & 7)
     code_ref[...] = jnp.where(wanted, (row << 15) | (local << 5) | used, 0)
-
-    high = iota((LISTED // 128, rows), 0)
-    low = iota((128, rows), 0)
+    total_ref[...] = jnp.zeros(total_ref.shape, f32)
+    height = LISTED // 128
+    sums = jnp.sum(held, axis=1, keepdims=True) + jnp.zeros((8, 128), f32)
+    list_ref[height : height + 8] = sums.astype(i32)
+
+
+def plan_collect(first, last, pos_ref, code_ref, total_ref):
+    rows = pos_ref.shape[1]
+    f32, bf16, i32 = jnp.float32, jnp.bfloat16, jnp.int32
+    high = lax.broadcasted_iota(i32, (LISTED // 128, rows), 0)
+    low = lax.broadcasted_iota(i32, (128, rows), 0)
 
     def collect(s, total):
         p = pos_ref[pl.ds(s, 1)]
         c = code_ref[pl.ds(s, 1)]
         hit = high == (p >> 7)
-        bytes_of = [jnp.where(hit, ((c >> (8 * k)) & 255).astype(f32), 0.0) for k in range(4)]
-        left = jnp.concatenate(bytes_of, axis=0).astype(bf16)
-        right = ones(low == (p & 127)).astype(bf16)
+        left = [jnp.where(hit, ((c >> (8 * k)) & 255).astype(f32), 0.0) for k in range(4)]
+        left = jnp.concatenate(left, axis=0).astype(bf16)
+        right = jnp.where(low == (p & 127), 1.0, 0.0).astype(bf16)
         return total + lax.dot_general(
             left, right, (((1,), (1,)), ((), ())), preferred_element_type=f32
         )
 
+    total_ref[...] = lax.fori_loop(first, last, collect, total_ref[...])
+
+
+def plan_finish(list_ref, total_ref, rows):
     height = LISTED // 128
-    total = lax.fori_loop(0, slots, collect, jnp.zeros((4 * height, 128), f32)).astype(i32)
+    total = total_ref[...].astype(jnp.int32)
     out = total[:height]
     for k in range(1, 4):
         out = out + total[k * height : (k + 1) * height] * (1 << (8 * k))
     list_ref[0:height] = jnp.where(out == 0, rows << 15, out)
-    sums = jnp.where(
-        iota((8, 128), 0) == 0, jnp.sum(some, axis=1, keepdims=True),
-        jnp.sum(extra, axis=1, keepdims=True),
-    )
-    list_ref[height : height + 8] = sums.astype(i32)
 
 
 def gather_kernel(
-    sizes, q_ref, table_ref, len_ref, all_ref, list_ref, pos_ref, code_ref, own_sem, send, recv
+    sizes, q_ref, table_ref, len_ref, all_ref, list_ref, pos_ref, code_ref, total_ref, own_sem,
+    send, recv
 ):
     side, y, z = place()
 
@@ -192,10 +223,21 @@
     greet(near())
     for copy in own:
         copy.wait()
-    torus_gather(
-        view, send, recv,
-        lambda: plan(sizes, table_ref, len_ref, list_ref, pos_ref, code_ref),
-    )
+    slots, rows = table_ref.shape
+
+    def between(level, plane):
+        if level == 0:
+            plan_start(sizes, table_ref, len_ref, list_ref, pos_ref, code_ref, total_ref)
+        if level < 4:
+            plan_collect(
+                level * slots // 4, (level + 1) * slots // 4, pos_ref, code_ref, total_ref
+            )
+        else:
+            plan_finish(list_ref, total_ref, rows)
+            for j in range(RING):
+                plane(j)
+
+    torus_gather(view, send, recv, between)
 
 
 def gather_queries(queries, table, lengths, sizes):
@@ -211,7 +253,8 @@
         in_specs=[vmem] * 3,
         out_specs=(vmem, vmem),
         scratch_shapes=[
-            pltpu.VMEM(table.shape, jnp.int32), pltpu.VMEM(table.shape, jnp.int32), dma((4,)),
+            pltpu.VMEM(table.shape, jnp.int32), pltpu.VMEM(table.shape, jnp.int32),
+            pltpu.VMEM((LISTED // 32, 128), jnp.float32), dma((4,)),
         ] + torus_sems(),
         compiler_params=pltpu.CompilerParams(collective_id=0, has_side_effects=True, vmem_limit_bytes=8 << 20),
         cost_estimate=pl.CostEstimate(flops=20_000_000_000, bytes_accessed=8 << 20, transcendentals=0),
@@ -269,14 +312,17 @@
         ]
         soft_of = [soft(x, h[4]) for x, h in zip(scores, halves)]
         none = jnp.zeros((tall, wide), jnp.bfloat16)
-        left = jnp.concatenate([
-            jnp.concatenate([x[2], none] if k % 2 == 0 else [none, x[2]], axis=1)
-            for k, x in enumerate(soft_of)
-        ], axis=0)
-        right = jnp.concatenate([
-            jnp.concatenate([halves[k][3], halves[k + 1][3]], axis=0)
-            for k in range(0, len(halves), 2)
-        ], axis=1)
+        if len(halves) == 1:
+            left, right = soft_of[0][2], halves[0][3]
+        else:
+            left = jnp.concatenate([
+                jnp.concatenate([x[2], none] if k % 2 == 0 else [none, x[2]], axis=1)
+                for k, x in enumerate(soft_of)
+            ], axis=0)
+            right = jnp.concatenate([
+                jnp.concatenate([halves[k][3], halves[k + 1][3]], axis=0)
+                for k in range(0, len(halves), 2)
+            ], axis=1)
         acc = jnp.dot(left, right, preferred_element_type=f32)
         out = []
         for k in range(len(halves)):
@@ -292,37 +338,46 @@
         mass_here = stat_lane == ((row >> 3) & 3) * 2 + 1
         return row >> 5, row & 31, pl.ds(first, q_local), peak_here, mass_here
 
-    first_count = listed[LISTED]
-    more_count = listed[LISTED + 128]
-    step = GROUP * UNROLL
-
-    @pl.loop(0, (first_count + step - 1) // step)
+    def batch(first):
+        parts = []
+        for k in range(0, BATCH, 4 * GROUP):
+            parts += quad([first + k + u * GROUP for u in range(4)])
+        return parts
+
+    def put(row, peak, mass, acc):
+        block, at, lines, peak_here, mass_here = split(row)
+        acc_ref[block, at] = acc
+        pltpu.store(
+            stat_ref.at[block, lines], jnp.where(peak_here, peak, mass), mask=peak_here | mass_here
+        )
+
+    def merged(row, peak, mass, acc):
+        block, at, lines, peak_here, mass_here = split(row)
+        old = stat_ref[block, lines]
+        old_peak = jnp.max(jnp.where(peak_here, old, NEG), axis=1, keepdims=True)
+        old_mass = jnp.sum(jnp.where(mass_here, old, 0.0), axis=1, keepdims=True)
+        top = jnp.maximum(old_peak, peak)
+        old_f = jnp.exp(old_peak - top)
+        new_f = jnp.exp(peak - top)
+        return row, top, old_mass * old_f + mass * new_f, acc_ref[block, at] * old_f + acc * new_f
+
+    @pl.loop(0, (listed[LISTED] + BATCH - 1) // BATCH)
     def _(i):
-        parts = []
-        for u in range(0, UNROLL, 4):
-            parts += quad([i * step + (u + k) * GROUP for k in range(4)])
-        for row, peak, mass, acc in parts:
-            block, at, lines, peak_here, mass_here = split(row)
-            acc_ref[block, at] = acc
-            stat_ref[block, lines] = jnp.where(
-                peak_here, peak, jnp.where(mass_here, mass, stat_ref[block, lines])
-            )
-
-    @pl.loop(0, (more_count + 2 * GROUP - 1) // (2 * GROUP))
+        for part in batch(i * BATCH):
+            put(*part)
+
+    for count, first, by in (
+        (listed[LISTED + 128], SECOND - BATCH, -BATCH), (listed[LISTED + 256], THIRD, BATCH),
+    ):
+        @pl.loop(0, (count + BATCH - 1) // BATCH)
+        def _(i):
+            for part in [merged(*part) for part in batch(first + i * by)]:
+                put(*part)
+
+    @pl.loop(0, (listed[LISTED + 384] + GROUP - 1) // GROUP)
     def _(i):
-        parts = quad([LISTED - GROUP - i * 2 * GROUP, LISTED - 2 * GROUP - i * 2 * GROUP])
-        for row, peak, mass, acc in parts:
-            block, at, lines, peak_here, mass_here = split(row)
-            old = stat_ref[block, lines]
-            old_peak = jnp.max(jnp.where(peak_here, old, NEG), axis=1, keepdims=True)
-            old_mass = jnp.sum(jnp.where(mass_here, old, 0.0), axis=1, keepdims=True)
-            top = jnp.maximum(old_peak, peak)
-            old_f = jnp.exp(old_peak - top)
-            new_f = jnp.exp(peak - top)
-            acc_ref[block, at] = acc_ref[block, at] * old_f + acc * new_f
-            stat_ref[block, lines] = jnp.where(
-                peak_here, top, jnp.where(mass_here, old_mass * old_f + mass * new_f, old)
-            )
+        for part in quad([LATER + i * GROUP]):
+            put(*merged(*part))
 
     eighth = 128 // q_local
 
@@ -358,7 +413,7 @@
 def finish_kernel(
     acc_hbm, stat_hbm, w_hbm, att_out, proj_out,
     got_acc, got_stat, out_code, out_stat, in_code, in_stat,
-    last_code, last_stat, weight, mixed, everyone, part_out, part_step_out, part_in, part_step_in,
+    last_code, last_stat, weight, mixed, everyone, own_part, part_out, part_step_out, part_in, part_step_in,
     cross_send, cross_recv, hop_send, hop_recv, last_send, last_recv, w_sem,
     part_send, part_recv,
     torus_send, torus_recv,
@@ -370,7 +425,6 @@
     side, y, z = place()
     rows, q_local, head_dim = att_out.shape
     out_rows = proj_out.shape[0]
-    half_width = proj_out.shape[1] // 2
     f32 = jnp.float32
     load_w = pltpu.make_async_copy(w_hbm, weight, w_sem)
     load_w.start()
@@ -488,7 +542,7 @@
     @pl.loop(0, 4)
     def _(q):
         gathered(3, q, (1, 2))
-        for o in (1, 3, 2):
+        for o in (2, 1, 3):
             for copy in last_copies(o, q):
                 copy.start()
 
@@ -511,60 +565,59 @@
         at = (h % 4) * head_dim
         everyone[me, h // 4, :, at : at + head_dim] = mixed[:, h, :].astype(jnp.bfloat16)
 
-    torus_gather(lambda q, of, at_y, at_z: everyone.at[spot(of, at_y, at_z), q], torus_send, torus_recv)
-    load_w.wait()
-
     band = q_local * head_dim // 4
     homes = n // m
 
-    def rows_of(i):
-        at = pl.multiple_of(lax.rem(mine + i + m, m) * homes, homes)
+    def part_copies(j, slot):
+        target = {"mp": around(z + j)}
+        return (
+            remote(part_out.at[j], part_in.at[slot], part_send.at[0, j], part_recv.at[0, slot], target),
+            remote(part_step_out.at[j], part_step_in.at[slot], part_send.at[1, j],
+                   part_recv.at[1, slot], target),
+        )
+
+    def project(j):
+        owner = around(z + j)
+        at = pl.multiple_of(owner * homes, homes)
         value = 0.0
         for q in range(4):
             value += jnp.dot(
                 everyone[pl.ds(at, homes), q].reshape(out_rows, band),
                 weight[q * band : (q + 1) * band], preferred_element_type=f32,
             )
-        return value
-
-    def side_copies(kind, half):
-        by = 1 - 2 * half
-        peer = {"mp": lax.rem(mine + (m - by if kind == 1 else by) + m, m)}
-        return (
-            remote(part_out.at[kind, half], part_in.at[kind, half], part_send.at[0, kind, half],
-                   part_recv.at[0, kind, half], peer),
-            remote(part_step_out.at[kind, half], part_step_in.at[kind, half],
-                   part_send.at[1, kind, half], part_recv.at[1, kind, half], peer),
-        )
-
-    def put(kind, half, value):
-        part_out[kind, half], step = encode(value)
-        part_step_out[kind, half, 0:1] = step
-        for copy in side_copies(kind, half):
-            copy.start()
-
-    def arrived(kind, half):
-        for copy in side_copies(kind, half):
+
+        @pl.when(owner == mine)
+        def _():
+            own_part[...] = value
+
+        @pl.when(owner != mine)
+        def _():
+            part_out[j], step = encode(value)
+            part_step_out[j, 0:1] = step
+            for copy in part_copies(j, around(mine - owner)):
+                copy.start()
+
+    def between(level, plane):
+        if level == 1:
+            load_w.wait()
+        for j in {2: (0,), 3: (1, 3), 4: (2,)}.get(level, ()):
+            plane(j)
+            project(j)
+
+    torus_gather(
+        lambda q, of, at_y, at_z: everyone.at[spot(of, at_y, at_z), q], torus_send, torus_recv,
+        between,
+    )
+    total = own_part[...]
+    for slot in range(1, m):
+        for copy in part_copies(0, slot):
             copy.wait_recv()
-        return part_in[kind, half].astype(f32) * part_step_in[kind, half, 0:1]
-
-    halves = [slice(0, half_width), slice(half_width, 2 * half_width)]
-    value = rows_of(2)
-    for half in range(2):
-        put(0, half, value[:, halves[half]])
-    before = rows_of(-1)
-    put(1, 0, before[:, halves[0]])
-    after = rows_of(1)
-    put(1, 1, after[:, halves[1]])
-    put(2, 0, after[:, halves[0]] + arrived(0, 0))
-    put(2, 1, before[:, halves[1]] + arrived(0, 1))
-    value = rows_of(0)
-    for half in range(2):
-        total = value[:, halves[half]] + arrived(1, half) + arrived(2, half)
-        proj_out[:, halves[half]] = total.astype(jnp.bfloat16)
-    for kind in range(3):
-        for half in range(2):
-            for copy in side_copies(kind, half):
+        total = total + part_in[slot].astype(f32) * part_step_in[slot, 0:1]
+    proj_out[...] = total.astype(jnp.bfloat16)
+    for j in range(m):
+        @pl.when(around(z + j) != mine)
+        def _():
+            for copy in part_copies(j, 1):
                 copy.wait_send()
 
     @pl.loop(0, 16)
@@ -608,13 +661,14 @@
             pltpu.VMEM((depth, columns), out_weight.dtype),
             pltpu.VMEM((rows, q_local, head_dim), f32),
             pltpu.VMEM((n, 4, rows, q_local * head_dim // 4), jnp.bfloat16),
-            pltpu.VMEM((3, 2, out_rows, columns // 2), i16),
-            pltpu.VMEM((3, 2, 8, columns // 2), f32),
-            pltpu.VMEM((3, 2, out_rows, columns // 2), i16),
-            pltpu.VMEM((3, 2, 8, columns // 2), f32),
+            pltpu.VMEM((out_rows, columns), f32),
+            pltpu.VMEM((m, out_rows, columns), i16),
+            pltpu.VMEM((m, 8, columns), f32),
+            pltpu.VMEM((m, out_rows, columns), i16),
+            pltpu.VMEM((m, 8, columns), f32),
             dma((2, 4, 4)), dma((2, 4, 4)),
             dma((2, 3, 4)), dma((2, 3, 4)), dma((2, 3, 4)), dma((2, 3, 4)), dma,
-            dma((2, 3, 2)), dma((2, 3, 2)),
+            dma((2, m)), dma((2, m)),
         ] + torus_sems(),
         compiler_params=pltpu.CompilerParams(collective_id=1, has_side_effects=True, vmem_limit_bytes=24 << 20),
     )(acc, stat, out_weight)

time: 105 us -> 96.4 us (0.918); the launches traced: 103 us -> 96.3 us
  Pallas kernels: 98.9 us -> 91.8 us
    pallas_call x1, Pallas kernels: 20.1 us -> 14.3 us  [attend(): pl.pallas_call(functools.partial(attend_kernel, (kv_local, blocks)), out_...]
    pallas_call x1, Pallas kernels: 27.8 us -> 24.7 us  [gather_queries(): pl.pallas_call(functools.partial(gather_kernel, sizes), out_shape=(jax.Sh...]
    pallas_call x1, Pallas kernels: 51 us -> 52.7 us  [finish(): pl.pallas_call(finish_kernel, out_shape=(jax.ShapeDtypeStruct((rows, q_lo...]
where the time goes in v1:
time: 96.4 us; the launch traced here: 96.3 us
  Pallas kernels  91.8 us (95%)
  local copies, waits for them, and re-layouts  3.81 us (4%)
    pallas_call x1, Pallas kernels, finish(): pl.pallas_call(finish_kernel, out_shape=(jax.ShapeDtypeStruct((rows, q_lo...  52.7 us
    pallas_call x1, Pallas kernels, gather_queries(): pl.pallas_call(functools.partial(gather_kernel, sizes), out_shape=(jax.Sh...  24.7 us
    pallas_call x1, Pallas kernels, attend(): pl.pallas_call(functools.partial(attend_kernel, (kv_local, blocks)), out_...  14.3 us
    unnamed x14, local copies, waits for them, and re-layouts  3.81 us

profile of v1, /device:TPU:4, one launch (start us, length us, event | category | flops | bytes accessed | tf_op | source)
XLA Modules:
  0.0 96.3 jit_solution(15544027233596240270)
XLA Ops:
  0.6 0.0 copy-start.3
  0.6 0.9 copy-done.3
  1.5 0.0 copy-start.4
  1.5 0.9 copy-done.4
  2.4 0.0 copy-start.5
  2.4 0.7 copy-done.5
  3.1 0.0 copy-start
  3.1 0.0 copy-start.1
  3.1 24.7 %shard_map.77 = (bf16[4,4,2,4,8,16,128]{6,5,4,3,2,1,0:T(8,128)(2,1)S(1)}, s32[40,128]{1,0:T(8,128)S(1)}) custom-call(bf16[4,8,16,128]{3,2,1,0:T(8,128)(2,1)S(1)} %bitcast.11, s32[32,1024]{1,0:T(8,128)S(1)} %bitcast.12, s32[1,1024]{1,0:T(1,128)S(1)} %bitcast.13), custom_call_target="tpu_custom_call" | custom-call | flops 20000000000 | bytes 8388608 | tf_op jit(solution)/shard_map/pallas_call | solution.py:247
  27.9 0.0 copy-done
  27.9 0.0 copy-done.1
  27.9 0.0 copy-start.2
  27.9 14.3 %shard_map.78 = (f32[32,4,128,128]{3,2,1,0:T(8,128)S(1)}, f32[32,8,128]{2,1,0:T(8,128)S(1)}) custom-call(s32[5120]{0:T(1024)S(1)} %bitcast.10, bf16[1024,16,128]{2,1,0:T(8,128)(2,1)S(1)} %bitcast.9, bf16[1024,32,128]{2,1,0:T(8,128)(2,1)S(1)} %bitcast.7, bf16[1024,32,128]{2,1,0:T(8,128)(2,1)S(1)} %bitcast.8), custom_call_target="tpu_custom_call" | custom-call | tf_op jit(solution)/shard_map/pallas_call | solution.py:397
  42.2 0.0 copy-done.2
  42.2 52.7 %shard_map.79 = (bf16[32,16,128]{2,1,0:T(8,128)(2,1)S(1)}, bf16[256,256]{1,0:T(8,128)(2,1)S(1)}) custom-call(f32[32,4,128,128]{3,2,1,0:T(8,128)S(1)} %get-tuple-element.8.acc_hbm, f32[32,8,128]{2,1,0:T(8,128)S(1)} %get-tuple-element.9.stat_hbm, bf16[2048,256]{1,0:T(8,128)(2,1)S(1)} %copy-done.2), custom_call_target="tpu_custom_call" | custom-call | tf_op jit(solution)/shard_map/pallas_call | solution.py:644
  95.0 0.7 copy.10
  95.6 0.7 copy.11
Async XLA Ops:
  0.6 0.9 copy-start.3
  1.5 0.9 copy-start.4
  2.4 0.7 copy-start.5
  3.1 24.8 %copy-start = (bf16[1024,16,2,128]{3,2,1,0:T(2,128)(2,1)S(1)}, bf16[1024,16,2,128]{3,2,1,0:T(2,128)(2,1)}, u32[]{:S(2)}) copy-start(bf16[1024,16,2,128]{3,2,1,0:T(2,128)(2,1)} %param.7) | copy-start | bytes 25165828
  3.1 24.8 %copy-start.1 = (bf16[1024,16,2,128]{3,2,1,0:T(2,128)(2,1)S(1)}, bf16[1024,16,2,128]{3,2,1,0:T(2,128)(2,1)}, u32[]{:S(2)}) copy-start(bf16[1024,16,2,128]{3,2,1,0:T(2,128)(2,1)} %param.8) | copy-start | bytes 25165828
  27.9 14.3 %copy-start.2 = (bf16[2048,256]{1,0:T(8,128)(2,1)S(1)}, bf16[2048,256]{1,0:T(8,128)(2,1)}, u32[]{:S(2)}) copy-start(bf16[2048,256]{1,0:T(8,128)(2,1)} %w_hbm.1) | copy-start | bytes 3145732
